TPU v7x, 32 devices: a whole 2x2x4 slice. The times are simulated.
32 devices in a mesh: groups: 2 (over y), expert: 4 (over z), tensor: 4 (over x, core).
Axes of the slice: x: 2, y: 2, z: 4, core: 2. Of those that a mesh axis runs over, the one named last changes fastest.
Arguments:
- tokens: bfloat16 [256, 4096], P(('groups', 'expert'), 'tensor'), parts along dimension 0, may hold values from -6 to 6
- expert_ids: int32 [256, 8], P(('groups', 'expert')), parts along dimension 0, may hold values from 0 to 63, all different within a row; in each aligned block of 32 rows (0 to 31, 32 to 63, ...) at most 8 rows name the same one
- gate_fixed: int32 [256, 8], P(('groups', 'expert')), parts along dimension 0, may hold values from 1 to 65535
- w_gate: bfloat16 [64, 4096, 768], P('expert', None, 'tensor'), may hold values from -0.09375 to 0.09375
- w_up: bfloat16 [64, 4096, 768], P('expert', None, 'tensor'), may hold values from -0.09375 to 0.09375
- w_down: bfloat16 [64, 768, 4096], P('expert', 'tensor'), may hold values from -0.21875 to 0.21875
Outputs:
- mixed: bfloat16 [256, 4096], P(('groups', 'expert'), 'tensor'), parts along dimension 0
There are 2 independent parts, one for each index of `groups`. A program takes and returns all parts, laid end to end along the dimension named above; an argument that names none is the same for every part. Nothing has to cross between parts.
Inputs may be any that keep to these rules, and one draw needn't show every extreme that they name: `expert_ids`: each row names 8 different experts. Within the 32 rows of one index of the expert axis no expert is named more than 8 times, and in every draw some expert is named exactly 8 times in some such block.
All inputs are finite; a program needn't handle non-finite values.
Results may differ from a plain program's by a relative error of at most 0.014.
Values may be sent and summed in bfloat16 or wider, within the bound.
A program may use at most 128 MiB of HBM per device.

v0:
```python
import jax
import jax.numpy as jnp
from jax import lax
from jax.sharding import PartitionSpec as P

CAP = 8


def expert_block(slot_rows, w_gate, w_up, w_down):
    gate_proj = jnp.einsum("gekd,edf->gekf", slot_rows, w_gate, preferred_element_type=jnp.float32)
    up_proj = jnp.einsum("gekd,edf->gekf", slot_rows, w_up, preferred_element_type=jnp.float32)
    hidden = (jax.nn.silu(gate_proj) * up_proj).astype(jnp.bfloat16)
    partial_value = jnp.einsum("gekf,efd->gekd", hidden, w_down, preferred_element_type=jnp.float32)
    summed = lax.psum_scatter(
        partial_value.astype(jnp.bfloat16), "tensor", scatter_dimension=3, tiled=True
    )
    return lax.all_to_all(summed, "expert", split_axis=0, concat_axis=0, tiled=True)


def on_device(tokens, expert_ids, gate_fixed, w_gate, w_up, w_down):
    tok_rows, per_token = expert_ids.shape
    local_experts = w_gate.shape[0]
    devices_e = lax.axis_size("expert")
    experts = local_experts * devices_e
    capacity = CAP
    flat_ids = expert_ids.reshape(-1)
    pick_count = tok_rows * per_token
    onehot = (flat_ids[:, None] == jnp.arange(experts, dtype=jnp.int32)[None, :]).astype(jnp.int32)
    before = jnp.cumsum(onehot, axis=0) - onehot
    slot_rank = jnp.sum(before * onehot, axis=1)
    slot_index = flat_ids * capacity + slot_rank
    owner_row = jnp.arange(pick_count, dtype=jnp.int32) // per_token
    slot_token = jnp.full((experts * capacity,), tok_rows, jnp.int32).at[slot_index].set(owner_row)
    padded = jnp.concatenate([tokens, jnp.zeros((1, tokens.shape[1]), tokens.dtype)], axis=0)
    returned = expert_block(
        lax.all_gather(
            lax.all_to_all(
                padded[slot_token].reshape(devices_e, local_experts, capacity, tokens.shape[1]),
                "expert",
                split_axis=0,
                concat_axis=0,
                tiled=True,
            ),
            "tensor",
            axis=3,
            tiled=True,
        ),
        w_gate,
        w_up,
        w_down,
    )
    flat_returned = returned.reshape(experts * capacity, returned.shape[3])
    picked = flat_returned[slot_index].reshape(tok_rows, per_token, returned.shape[3])
    weights = gate_fixed.astype(jnp.float32)
    gate_share = weights / jnp.sum(weights, axis=1, keepdims=True)
    mixed_out = jnp.einsum("tk,tkf->tf", gate_share, picked.astype(jnp.float32))
    return mixed_out.astype(jnp.bfloat16)


def solution(mesh):
    placed = (
        P(("groups", "expert"), "tensor"),
        P(("groups", "expert"), None),
        P(("groups", "expert"), None),
        P("expert", None, "tensor"),
        P("expert", None, "tensor"),
        P("expert", "tensor", None),
    )
    return jax.shard_map(
        on_device,
        mesh=mesh,
        in_specs=placed,
        out_specs=P(("groups", "expert"), "tensor"),
        check_vma=False,
    )
```

profile of v0, /device:TPU:0, one launch (start us, length us, event | category | flops | bytes accessed | tf_op | source)
XLA Modules:
  0.0 207.7 jit_solution(213641463679312116)
XLA Ops:
  6.5 0.0 all-gather.2.cloned.1.call-start
  6.5 0.8 copy.14
  7.3 0.1 eq.29
  7.4 0.1 eq.25
  7.5 0.7 broadcast_multiply_fusion
  8.2 0.6 reduce-window.6
  8.8 0.2 slice_reduce_fusion
  9.0 0.1 copy.13
  9.1 0.1 mul.28
  9.2 0.1 fusion.28
  9.3 1.4 scatter_custom_fusion
  10.7 0.8 concatenate.3
  11.6 2.0 gather_fusion
  13.7 31.9 %all_to_all.10 = bf16[4,16,8,1024]{3,2,1,0:T(8,128)(2,1)S(1)} all-to-all(bf16[4,16,8,1024]{3,2,1,0:T(8,128)(2,1)S(1)} %bitcast.73), channel_id=1, replica_groups=mesh['groups'=2,'expert'=4,'tensor'=4] {'expert'}, dimensions={0} | all-to-all | bytes 2097152 | tf_op jit(solution)/shard_map/all_to_all | solution.py:37
  45.5 1.1 copy.17
  46.6 0.0 all-gather.2.cloned.1.call-update
  46.6 0.0 reduce-scatter.2.cloned.1.call-start
  46.7 33.7 %all-gather.2.cloned.1.call-done = bf16[4,16,8,4096]{3,2,0,1:T(8,128)(2,1)} async-done(((bf16[4,16,8,1024]{3,2,0,1:T(8,128)(2,1)}), bf16[4,16,8,4096]{3,2,0,1:T(8,128)(2,1)}) %all-gather.2.cloned.1.call-update) | async-done | bytes 4194320 | tf_op jit(solution)/shard_map/all_gather | solution.py:36
  80.3 13.2 %fusion.12 = f32[4,16,8,192]{3,2,0,1:T(8,128)S(1)} fusion(bf16[4,16,8,4096]{3,2,0,1:T(8,128)(2,1)} %all-gather.2.cloned.1.call-done, bf16[16,4096,192]{1,2,0:T(8,128)(2,1)} %param.9), kind=kOutput, calls=%fused_computation.11 | convolution fusion | flops 805306368 | bytes 29753344 | tf_op jit(solution)/shard_map/gekd,edf->gekf/dot_general | solution.py:10
  93.6 13.4 %fusion.21 = bf16[4,16,8,192]{3,2,0,1:T(8,128)(2,1)S(1)} fusion(bf16[4,16,8,4096]{3,2,0,1:T(8,128)(2,1)} %all-gather.2.cloned.1.call-done, bf16[16,4096,192]{1,2,0:T(8,128)(2,1)} %param.10, f32[4,16,8,192]{3,2,0,1:T(8,128)S(1)} %fusion.12), kind=kOutput, calls=%fused_computation.14 | convolution fusion | flops 805896192 | bytes 29949952 | tf_op jit(solution)/shard_map/gekd,edf->gekf/dot_general | solution.py:11
  107.0 0.0 copy-start
  107.0 14.6 %fusion.9 = bf16[4,16,8,4096]{3,2,0,1:T(8,128)(2,1)} fusion(bf16[4,16,8,192]{3,2,0,1:T(8,128)(2,1)S(1)} %fusion.21, bf16[16,192,4096]{2,1,0:T(8,128)(2,1)} %param.11), kind=kOutput, calls=%fused_computation.10 | convolution fusion | flops 807403520 | bytes 29556736 | tf_op jit(solution)/shard_map/gekf,efd->gekd/dot_general | solution.py:13
  121.7 0.0 reduce-scatter.2.cloned.1.call-update
  121.7 44.6 %reduce-scatter.2.cloned.1.call-done = bf16[4,16,8,1024]{3,2,0,1:T(8,128)(2,1)} async-done(((bf16[4,16,8,4096]{3,2,0,1:T(8,128)(2,1)}), bf16[4,16,8,1024]{3,2,0,1:T(8,128)(2,1)}) %reduce-scatter.2.cloned.1.call-update) | async-done | bytes 1048592 | tf_op jit(solution)/shard_map/reduce_scatter | solution.py:14
  166.3 2.3 %copy.18 = bf16[4,16,8,1024]{3,2,1,0:T(8,128)(2,1)} copy(bf16[4,16,8,1024]{3,2,0,1:T(8,128)(2,1)} %reduce-scatter.2.cloned.1.call-done) | data formatting | bytes 2097152 | tf_op jit(solution)/shard_map/reduce_scatter | solution.py:14
  168.6 4.6 %all-to-all-start.1 = ((bf16[4,16,8,1024]{3,2,1,0:T(8,128)(2,1)}), bf16[4,16,8,1024]{3,2,1,0:T(8,128)(2,1)S(1)}, u32[]{:S(2)}, u32[]{:S(2)}) async-start(bf16[4,16,8,1024]{3,2,1,0:T(8,128)(2,1)} %copy.18), calls=%async_computation.2 | async-start | bytes 2097152 | tf_op jit(solution)/shard_map/all_to_all | solution.py:17
  173.2 0.0 copy-done
  173.2 0.1 copy.22
  173.3 25.4 %all-to-all-done.1 = bf16[4,16,8,1024]{3,2,1,0:T(8,128)(2,1)S(1)} async-done(((bf16[4,16,8,1024]{3,2,1,0:T(8,128)(2,1)}), bf16[4,16,8,1024]{3,2,1,0:T(8,128)(2,1)S(1)}, u32[]{:S(2)}, u32[]{:S(2)}) %all-to-all-start.1) | async-done | bytes 1048608 | tf_op jit(solution)/shard_map/all_to_all | solution.py:17
  198.7 1.2 gather_fusion.1
  199.9 0.3 fusion.24
  200.2 0.7 copy.27
  (10 shorter events, 0.1 us)
Async XLA Ops:
  6.5 73.8 %all-gather.2.cloned.1.call-start = ((), (), s32[]{:S(2)}) async-start(), calls=%async_computation.3 | async-start | bytes 5242880 | tf_op jit(solution)/shard_map/all_gather | solution.py:36
  46.6 119.6 %reduce-scatter.2.cloned.1.call-start = ((), (), s32[]{:S(2)}) async-start(), calls=%async_computation.4 | async-start | bytes 5242880 | tf_op jit(solution)/shard_map/reduce_scatter | solution.py:14
  107.0 66.2 %copy-start = (s32[32,8]{0,1:T(8,128)S(1)}, s32[32,8]{0,1:T(8,128)}, u32[]{:S(2)}) copy-start(s32[32,8]{0,1:T(8,128)} %param.8) | copy-start | bytes 3076
  168.6 30.1 %all-to-all-start.1 = ((bf16[4,16,8,1024]{3,2,1,0:T(8,128)(2,1)}), bf16[4,16,8,1024]{3,2,1,0:T(8,128)(2,1)S(1)}, u32[]{:S(2)}, u32[]{:S(2)}) async-start(bf16[4,16,8,1024]{3,2,1,0:T(8,128)(2,1)} %copy.18), calls=%async_computation.2 | async-start | bytes 2097152 | tf_op jit(solution)/shard_map/all_to_all | solution.py:17
Sparse Core Ops, SparseCore 0:
  46.7 33.5 all-gather.1
  121.8 44.4 reduce-scatter.1
where the time goes:
time: 208 us
  waiting for transfers between devices  104 us (50%)
  matrix products  41.6 us (20%)
  blocking collectives  31.9 us (15%)
  between operations  13.5 us (6%)
  local copies, waits for them, and re-layouts  10.9 us (5%)
  starting transfers between devices  4.64 us (2%)
    reduce_scatter x1, waiting for transfers between devices, expert_block(): lax.psum_scatter(partial_value.astype(jnp.bfloat16), 'tensor', scatter_di...  44.6 us
    all_gather x1, waiting for transfers between devices, on_device(): lax.all_gather(lax.all_to_all(padded[slot_token].reshape(devices_e, local...  33.7 us
    all_to_all x1, blocking collectives, on_device(): lax.all_to_all(padded[slot_token].reshape(devices_e, local_experts, capac...  31.9 us
    all_to_all x1, waiting for transfers between devices, expert_block(): lax.all_to_all(summed, 'expert', split_axis=0, concat_axis=0, tiled=True)  25.4 us
    dot_general x1, matrix products, expert_block(): jnp.einsum('gekf,efd->gekd', hidden, w_down, preferred_element_type=jnp.f...  14.6 us
    dot_general x1, matrix products, expert_block(): jnp.einsum('gekd,edf->gekf', slot_rows, w_up, preferred_element_type=jnp....  13.4 us
    dot_general x1, matrix products, expert_block(): jnp.einsum('gekd,edf->gekf', slot_rows, w_gate, preferred_element_type=jn...  13.2 us
    all_to_all x1, starting transfers between devices, expert_block(): lax.all_to_all(summed, 'expert', split_axis=0, concat_axis=0, tiled=True)  4.6 us
  transfers between devices with their start and end apart: 3, of which 3 were waited for; matrix products, arithmetic and copies ran while one was open for 0% of the time, Pallas kernels for 0%

commit v1 on v0

--- a/solution.py
+++ b/solution.py
@@ -1,6 +1,10 @@
+import functools
+
 import jax
 import jax.numpy as jnp
 from jax import lax
+from jax.experimental import pallas as pl
+from jax.experimental.pallas import tpu as pltpu
 from jax.sharding import PartitionSpec as P
 
 CAP = 8
@@ -17,7 +21,7 @@
     return lax.all_to_all(summed, "expert", split_axis=0, concat_axis=0, tiled=True)
 
 
-def on_device(tokens, expert_ids, gate_fixed, w_gate, w_up, w_down):
+def slotted(tokens, expert_ids, gate_fixed, w_gate, w_up, w_down):
     tok_rows, per_token = expert_ids.shape
     local_experts = w_gate.shape[0]
     devices_e = lax.axis_size("expert")
@@ -57,6 +61,286 @@
     return mixed_out.astype(jnp.bfloat16)
 
 
+MESH = pl.DeviceIdType.MESH
+VMEM_BYTES = 66_000_000
+
+
+def fused_kernel(
+    tok_rows, feats, experts, hidden_units, E, T,
+    x_ref, ids_ref, gates_ref, wg_ref, wu_ref, wd_ref, out_ref,
+    ring, down, tok, ids_all, gates_all, acc, hid_t, hid,
+    to_partner, from_partner, to_x, from_x, to_z, from_z, own,
+    w_sem, d_sem, own_sem, zt_send, zt_recv, zi_send, zi_recv, t_send, t_recv,
+    p_send, p_recv, x_send, x_recv, z_send, z_recv,
+):
+    g, e, t = lax.axis_index("groups"), lax.axis_index("expert"), lax.axis_index("tensor")
+    X = T // 2
+    x, c = lax.div(t, 2), lax.rem(t, 2)
+
+    def peer(k):
+        half, side = (k // 2, k % 2) if isinstance(k, int) else (lax.div(k, 2), lax.rem(k, 2))
+        return lax.rem(x + half, X) * 2 + lax.rem(c + side, 2)
+
+    def mirror(k):
+        return (-(k // 2)) % X * 2 + k % 2
+
+    def rows_of(block):
+        return pl.ds(pl.multiple_of(block * tok_rows, tok_rows), tok_rows)
+
+    def features_of(k):
+        return pl.ds(pl.multiple_of(peer(k) * feats, feats), feats)
+
+    pieces = down_pieces(experts, hidden_units)
+    piece_rows = experts * hidden_units // pieces
+
+    def weight_copies(k, i):
+        slot = (k % 2) * experts + i
+        return [
+            pltpu.make_async_copy(
+                w.at[i, :, features_of(k)],
+                ring.at[slot, pl.ds(part * hidden_units, hidden_units), :],
+                w_sem.at[slot, part],
+            )
+            for part, w in enumerate((wg_ref, wu_ref))
+        ]
+
+    def down_copy(k, piece):
+        rows = pl.ds(pl.multiple_of(piece * piece_rows, piece_rows), piece_rows)
+        return pltpu.make_async_copy(
+            wd_ref.at[rows, features_of(k)], down.at[k, rows, :], d_sem.at[k, piece]
+        )
+
+    for k in range(2):
+        @pl.loop(0, experts)
+        def _(i, k=k):
+            for copy in weight_copies(k, i):
+                copy.start()
+
+    barrier = pltpu.get_barrier_semaphore()
+    for d in range(1, E):
+        pl.semaphore_signal(barrier, inc=1, device_id=(g, lax.rem(e + d, E), t), device_id_type=MESH)
+    for k in range(1, T):
+        pl.semaphore_signal(barrier, inc=1, device_id=(g, e, peer(k)), device_id_type=MESH)
+    pl.semaphore_wait(barrier, E - 1 + T - 1)
+
+    def remote(src, dst, send, recv, where):
+        return pltpu.make_async_remote_copy(
+            src_ref=src, dst_ref=dst, send_sem=send, recv_sem=recv, device_id=where, device_id_type=MESH
+        )
+
+    sent = []
+
+    def go(*args):
+        copy = remote(*args)
+        copy.start()
+        sent.append(copy)
+
+    def arrived(dst, send, recv):
+        remote(dst, dst, send, recv, (g, e, peer(1))).wait_recv()
+
+    def spread(source, d):
+        block = lax.rem(e + E - d, E)
+        for k in [1] + [2 * dx for dx in range(1, X)]:
+            m = mirror(k)
+            go(source, tok.at[m, rows_of(block), :], t_send.at[k, d], t_recv.at[m, d], (g, e, peer(k)))
+
+    for d in range(1, E):
+        where = (g, lax.rem(e + d, E), t)
+        go(x_ref, tok.at[0, rows_of(e), :], zt_send.at[d], zt_recv.at[d], where)
+    spread(x_ref, 0)
+    for d in range(1, E):
+        where = (g, lax.rem(e + d, E), t)
+        go(ids_ref, ids_all.at[e], zi_send.at[0, d], zi_recv.at[0, d], where)
+        go(gates_ref, gates_all.at[e], zi_send.at[1, d], zi_recv.at[1, d], where)
+    local = [
+        pltpu.make_async_copy(x_ref, tok.at[0, rows_of(e), :], own_sem.at[0]),
+        pltpu.make_async_copy(ids_ref, ids_all.at[e], own_sem.at[1]),
+        pltpu.make_async_copy(gates_ref, gates_all.at[e], own_sem.at[2]),
+    ]
+    for copy in local:
+        copy.start()
+    for d in range(1, E):
+        landed = tok.at[0, rows_of(lax.rem(e + E - d, E)), :]
+        arrived(landed, zt_send.at[d], zt_recv.at[d])
+        spread(landed, d)
+    for copy in local:
+        copy.wait()
+
+    def project(k, i):
+        for copy in weight_copies(k, i):
+            copy.wait()
+        return lax.dot_general(
+            ring[(k % 2) * experts + i], tok[k], (((1,), (1,)), ((), ())), preferred_element_type=jnp.float32
+        )
+
+    for k in range(T):
+        if k == 1 or (k > 1 and k % 2 == 0):
+            for d in range(E):
+                block = lax.rem(e + E - d, E)
+                landed = tok.at[k, rows_of(block), :]
+                arrived(landed, t_send.at[k, d], t_recv.at[k, d])
+                if k > 1:
+                    go(landed, tok.at[k + 1, rows_of(block), :], t_send.at[k + 1, d], t_recv.at[k + 1, d], (g, e, peer(1)))
+        elif k > 1:
+            for d in range(E):
+                arrived(tok.at[k, rows_of(lax.rem(e + E - d, E)), :], t_send.at[k, d], t_recv.at[k, d])
+        if k == T - 1:
+            for d in range(1, E):
+                s = lax.rem(e + E - d, E)
+                arrived(ids_all.at[s], zi_send.at[0, d], zi_recv.at[0, d])
+                arrived(gates_all.at[s], zi_send.at[1, d], zi_recv.at[1, d])
+            ids = jnp.concatenate([ids_all[s] for s in range(E)], axis=1)
+            gates = jnp.concatenate([gates_all[s] for s in range(E)], axis=1).astype(jnp.float32)
+            share = gates / jnp.sum(gates, axis=0, keepdims=True)
+
+        @pl.loop(0, experts)
+        def _(i, k=k):
+            part = project(k, i)
+            if k == 0:
+                acc[i] = part
+            elif k < T - 1:
+                acc[i] += part
+            else:
+                both = acc[i] + part
+                gate, up = both[:hidden_units], both[hidden_units:]
+                weight = jnp.sum(jnp.where(ids == e * experts + i, share, 0.0), axis=0, keepdims=True)
+                value = gate / (1.0 + jnp.exp(-gate)) * up * weight
+                hid_t[pl.ds(pl.multiple_of(i * hidden_units, hidden_units), hidden_units), :] = value
+            if k + 2 < T:
+                for copy in weight_copies(k + 2, i):
+                    copy.start()
+            if k == 1:
+                for n in range(T * pieces // experts):
+                    j = i * (T * pieces // experts) + n
+                    order = lax.div(j, pieces)
+                    down_copy((T - 1) - order, lax.rem(j, pieces)).start()
+
+    pair = 2 * hidden_units
+
+    @pl.loop(0, experts // 2)
+    def _(i):
+        start = pl.multiple_of(i * pair, pair)
+        hid[:, pl.ds(start, pair)] = jnp.transpose(hid_t[pl.ds(start, pair), :]).astype(jnp.bfloat16)
+
+    width = min(256, feats)
+
+    def down_block(k, finish):
+        for piece in range(pieces):
+            down_copy(k, piece).wait()
+
+        @pl.loop(0, feats // width)
+        def _(n):
+            columns = pl.ds(pl.multiple_of(n * width, width), width)
+            finish(columns, jnp.dot(hid[...], down[k, :, columns], preferred_element_type=jnp.float32))
+
+    after_own = list(range(1, E)) + [0]
+    for dx in reversed(range(X)):
+        def keep(columns, value, dx=dx):
+            to_partner[dx, :, columns] = value.astype(jnp.bfloat16)
+
+        def store(columns, value):
+            own[:, columns] = value
+
+        down_block(2 * dx + 1, keep)
+        go(to_partner.at[dx], from_partner.at[dx], p_send.at[dx], p_recv.at[dx], (g, e, peer(1)))
+        down_block(2 * dx, store)
+        arrived(from_partner.at[dx], p_send.at[dx], p_recv.at[dx])
+        for j in after_own:
+            rows = rows_of(lax.rem(e + j, E))
+            total = own[rows, :] + from_partner[dx, rows, :].astype(jnp.float32)
+            if dx:
+                back = (X - dx) % X
+                to_x[dx, rows, :] = total.astype(jnp.bfloat16)
+                go(to_x.at[dx, rows, :], from_x.at[back, rows, :], x_send.at[dx, j], x_recv.at[back, j], (g, e, peer(2 * dx)))
+                continue
+            for other in range(1, X):
+                arrived(from_x.at[other, rows, :], x_send.at[other, j], x_recv.at[other, j])
+                total += from_x[other, rows, :].astype(jnp.float32)
+            if j:
+                to_z[j] = total.astype(jnp.bfloat16)
+                go(to_z.at[j], from_z.at[j], z_send.at[j], z_recv.at[j], (g, lax.rem(e + j, E), t))
+    for d in range(1, E):
+        arrived(from_z.at[d], z_send.at[d], z_recv.at[d])
+        total += from_z[d].astype(jnp.float32)
+    out_ref[...] = total.astype(out_ref.dtype)
+    for copy in sent:
+        copy.wait_send()
+
+
+def down_pieces(experts, hidden_units):
+    return 4 if experts % 4 == 0 and experts * hidden_units % 64 == 0 else 1
+
+
+def scratch_of(tok_rows, feats, experts, hidden_units, E, T, per_token):
+    bf16, f32, X, N = jnp.bfloat16, jnp.float32, T // 2, E * tok_rows
+    dma = pltpu.SemaphoreType.DMA
+    return [
+        ((2 * experts, 2 * hidden_units, feats), bf16),
+        ((T, experts * hidden_units, feats), bf16),
+        ((T, N, feats), bf16),
+        ((E, per_token, tok_rows), jnp.int32),
+        ((E, per_token, tok_rows), jnp.int32),
+        ((experts, 2 * hidden_units, N), f32),
+        ((experts * hidden_units, N), f32),
+        ((N, experts * hidden_units), bf16),
+        ((X, N, feats), bf16),
+        ((X, N, feats), bf16),
+        ((X, N, feats), bf16),
+        ((X, N, feats), bf16),
+        ((E, tok_rows, feats), bf16),
+        ((E, tok_rows, feats), bf16),
+        ((N, feats), f32),
+    ], [
+        dma((2 * experts, 2)), dma((T, down_pieces(experts, hidden_units))), dma((3,)),
+        dma((E,)), dma((E,)), dma((2, E)), dma((2, E)), dma((T, E)), dma((T, E)),
+        dma((X,)), dma((X,)), dma((X, E)), dma((X, E)), dma((E,)), dma((E,)),
+    ]
+
+
+def fits_fused(sizes):
+    tok_rows, feats, experts, hidden_units, E, T, per_token = sizes
+    if T % 2 or experts % 4 or E * tok_rows % 128 or feats % 256 or tok_rows % 16:
+        return False
+    if 2 * hidden_units % 128 or hidden_units % 16 or T * 4 % experts:
+        return False
+    buffers, _ = scratch_of(*sizes)
+    size = 0
+    for shape, kind in buffers:
+        count = jnp.dtype(kind).itemsize
+        for length in shape:
+            count *= length
+        size += count
+    return size < VMEM_BYTES - 2_000_000
+
+
+def on_device(tokens, expert_ids, gate_fixed, w_gate, w_up, w_down):
+    (tok_rows, feats), per_token = tokens.shape, expert_ids.shape[1]
+    experts, width, hidden_units = w_gate.shape
+    E, T = lax.axis_size("expert"), lax.axis_size("tensor")
+    sizes = (tok_rows, feats, experts, hidden_units, E, T, per_token)
+    if not fits_fused(sizes):
+        return slotted(tokens, expert_ids, gate_fixed, w_gate, w_up, w_down)
+    buffers, semaphores = scratch_of(*sizes)
+    vmem, anywhere = pl.BlockSpec(memory_space=pltpu.VMEM), pl.BlockSpec(memory_space=pl.ANY)
+    return pl.pallas_call(
+        functools.partial(fused_kernel, *sizes[:6]),
+        out_shape=jax.ShapeDtypeStruct(tokens.shape, tokens.dtype),
+        in_specs=[vmem, vmem, vmem, anywhere, anywhere, anywhere],
+        out_specs=vmem,
+        scratch_shapes=[pltpu.VMEM(shape, kind) for shape, kind in buffers] + semaphores,
+        compiler_params=pltpu.CompilerParams(
+            collective_id=0, has_side_effects=True, vmem_limit_bytes=VMEM_BYTES
+        ),
+    )(
+        tokens,
+        expert_ids.T,
+        gate_fixed.T,
+        jnp.swapaxes(w_gate, 1, 2),
+        jnp.swapaxes(w_up, 1, 2),
+        w_down.reshape(experts * hidden_units, width),
+    )
+
+
 def solution(mesh):
     placed = (
         P(("groups", "expert"), "tensor"),

time: 208 us -> 56.1 us (0.27)
  waiting for transfers between devices: 104 us -> 0 us
  Pallas kernels: 0 us -> 54.4 us
  matrix products: 41.6 us -> 0 us
  blocking collectives: 31.9 us -> 0 us
  between operations: 13.5 us -> 0.01 us
  local copies, waits for them, and re-layouts: 10.9 us -> 1.47 us
  starting transfers between devices: 4.64 us -> 0 us
    pallas_call x0 -> x1, Pallas kernels: none -> 54.4 us  [on_device(): pl.pallas_call(functools.partial(fused_kernel, *sizes[:6]), out_shape=jax...]
    reduce_scatter x1 -> x0, waiting for transfers between devices: 44.6 us -> none  [expert_block(): lax.psum_scatter(partial_value.astype(jnp.bfloat16), 'tensor', scatter_di...]
    dot_general x4 -> x0, matrix products: 41.6 us -> none  [the longest x1 14.6 us: expert_block(): jnp.einsum('gekf,efd->gekd', hidden, w_down, preferred_element_type=jnp.f...]
    all_gather x1 -> x0, waiting for transfers between devices: 33.7 us -> none  [on_device(): lax.all_gather(lax.all_to_all(padded[slot_token].reshape(devices_e, local...]
    all_to_all x1 -> x0, blocking collectives: 31.9 us -> none  [on_device(): lax.all_to_all(padded[slot_token].reshape(devices_e, local_experts, capac...]
    all_to_all x1 -> x0, waiting for transfers between devices: 25.4 us -> none  [expert_block(): lax.all_to_all(summed, 'expert', split_axis=0, concat_axis=0, tiled=True)]
    all_to_all x1 -> x0, starting transfers between devices: 4.6 us -> none  [expert_block(): lax.all_to_all(summed, 'expert', split_axis=0, concat_axis=0, tiled=True)]
    gather x2 -> x0, local copies, waits for them, and re-layouts: 3.22 us -> none  [the longest x1 2.05 us: on_device(): padded[slot_token]]
  transfers between devices with their start and end apart: 3 -> 0, of which waited for: 3 -> 0; matrix products, arithmetic and copies ran while one was open for 0% -> 0% of each run, Pallas kernels for 0% -> 0%
where the time goes in v1:
time: 56.1 us; the launch traced here: 55.9 us
  Pallas kernels  54.4 us (97%)
  local copies, waits for them, and re-layouts  1.47 us (3%)
    pallas_call x1, Pallas kernels, on_device(): pl.pallas_call(functools.partial(fused_kernel, *sizes[:6]), out_shape=jax...  54.4 us
    unnamed x1, local copies, waits for them, and re-layouts  1.47 us

profile of v1, /device:TPU:0, one launch (start us, length us, event | category | flops | bytes accessed | tf_op | source)
XLA Modules:
  0.0 55.9 jit_solution(2076033644936238107)
XLA Ops:
  0.0 54.4 %shard_map.64 = bf16[32,1024]{1,0:T(8,128)(2,1)} custom-call(bf16[32,1024]{1,0:T(8,128)(2,1)} %x_ref.1, s32[8,32]{1,0:T(8,128)} %bitcast.8, s32[8,32]{1,0:T(8,128)} %bitcast.9, bf16[16,192,4096]{2,1,0:T(8,128)(2,1)} %bitcast.5, bf16[16,192,4096]{2,1,0:T(8,128)(2,1)} %bitcast.6, bf16[3072,4096]{1,0:T(8,128)(2,1)} %bitcast.7), custom_call_target="tpu_custom_call" | custom-call | tf_op jit(solution)/shard_map/pallas_call | solution.py:325
  54.5 1.5 %copy.8 = bf16[32,1024]{1,0:T(8,128)(2,1)} copy(bf16[32,1024]{1,0:T(8,128)(2,1)} %shard_map.64) | data formatting | bytes 131072

commit v2 on v1

--- a/solution.py
+++ b/solution.py
@@ -63,6 +63,7 @@
 
 MESH = pl.DeviceIdType.MESH
 VMEM_BYTES = 66_000_000
+GROUP = 4
 
 
 def fused_kernel(
@@ -110,48 +111,6 @@
             wd_ref.at[rows, features_of(k)], down.at[k, rows, :], d_sem.at[k, piece]
         )
 
-    for k in range(2):
-        @pl.loop(0, experts)
-        def _(i, k=k):
-            for copy in weight_copies(k, i):
-                copy.start()
-
-    barrier = pltpu.get_barrier_semaphore()
-    for d in range(1, E):
-        pl.semaphore_signal(barrier, inc=1, device_id=(g, lax.rem(e + d, E), t), device_id_type=MESH)
-    for k in range(1, T):
-        pl.semaphore_signal(barrier, inc=1, device_id=(g, e, peer(k)), device_id_type=MESH)
-    pl.semaphore_wait(barrier, E - 1 + T - 1)
-
-    def remote(src, dst, send, recv, where):
-        return pltpu.make_async_remote_copy(
-            src_ref=src, dst_ref=dst, send_sem=send, recv_sem=recv, device_id=where, device_id_type=MESH
-        )
-
-    sent = []
-
-    def go(*args):
-        copy = remote(*args)
-        copy.start()
-        sent.append(copy)
-
-    def arrived(dst, send, recv):
-        remote(dst, dst, send, recv, (g, e, peer(1))).wait_recv()
-
-    def spread(source, d):
-        block = lax.rem(e + E - d, E)
-        for k in [1] + [2 * dx for dx in range(1, X)]:
-            m = mirror(k)
-            go(source, tok.at[m, rows_of(block), :], t_send.at[k, d], t_recv.at[m, d], (g, e, peer(k)))
-
-    for d in range(1, E):
-        where = (g, lax.rem(e + d, E), t)
-        go(x_ref, tok.at[0, rows_of(e), :], zt_send.at[d], zt_recv.at[d], where)
-    spread(x_ref, 0)
-    for d in range(1, E):
-        where = (g, lax.rem(e + d, E), t)
-        go(ids_ref, ids_all.at[e], zi_send.at[0, d], zi_recv.at[0, d], where)
-        go(gates_ref, gates_all.at[e], zi_send.at[1, d], zi_recv.at[1, d], where)
     local = [
         pltpu.make_async_copy(x_ref, tok.at[0, rows_of(e), :], own_sem.at[0]),
         pltpu.make_async_copy(ids_ref, ids_all.at[e], own_sem.at[1]),
@@ -159,19 +118,61 @@
     ]
     for copy in local:
         copy.start()
+    for k in range(2):
+        @pl.loop(0, experts)
+        def _(i, k=k):
+            for copy in weight_copies(k, i):
+                copy.start()
+
+    barrier = pltpu.get_barrier_semaphore()
+    for d in range(1, E):
+        pl.semaphore_signal(barrier, inc=1, device_id=(g, lax.rem(e + d, E), t), device_id_type=MESH)
+    for k in range(1, T):
+        pl.semaphore_signal(barrier, inc=1, device_id=(g, e, peer(k)), device_id_type=MESH)
+    pl.semaphore_wait(barrier, E - 1 + T - 1)
+
+    def remote(src, dst, send, recv, where):
+        return pltpu.make_async_remote_copy(
+            src_ref=src, dst_ref=dst, send_sem=send, recv_sem=recv, device_id=where, device_id_type=MESH
+        )
+
+    for copy in local:
+        copy.wait()
+    held = tok.at[0, rows_of(e), :]
+    sent = []
+
+    def go(*args):
+        copy = remote(*args)
+        copy.start()
+        sent.append(copy)
+
+    def arrived(dst, send, recv):
+        remote(dst, dst, send, recv, (g, e, peer(1))).wait_recv()
+
+    def spread(source, d):
+        block = lax.rem(e + E - d, E)
+        for k in [1] + [2 * dx for dx in range(1, X)]:
+            m = mirror(k)
+            go(source, tok.at[m, rows_of(block), :], t_send.at[k, d], t_recv.at[m, d], (g, e, peer(k)))
+
+    for d in range(1, E):
+        where = (g, lax.rem(e + d, E), t)
+        go(held, held, zt_send.at[d], zt_recv.at[d], where)
+    spread(held, 0)
+    for d in range(1, E):
+        where = (g, lax.rem(e + d, E), t)
+        go(ids_all.at[e], ids_all.at[e], zi_send.at[0, d], zi_recv.at[0, d], where)
+        go(gates_all.at[e], gates_all.at[e], zi_send.at[1, d], zi_recv.at[1, d], where)
     for d in range(1, E):
         landed = tok.at[0, rows_of(lax.rem(e + E - d, E)), :]
         arrived(landed, zt_send.at[d], zt_recv.at[d])
         spread(landed, d)
-    for copy in local:
-        copy.wait()
-
     def project(k, i):
-        for copy in weight_copies(k, i):
-            copy.wait()
-        return lax.dot_general(
-            ring[(k % 2) * experts + i], tok[k], (((1,), (1,)), ((), ())), preferred_element_type=jnp.float32
-        )
+        for n in range(GROUP):
+            for copy in weight_copies(k, i + n):
+                copy.wait()
+        rows = ring[pl.ds((k % 2) * experts + i, GROUP)].reshape(GROUP * 2 * hidden_units, feats)
+        return lax.dot_general(rows, tok[k], (((1,), (1,)), ((), ())), preferred_element_type=jnp.float32)
 
     for k in range(T):
         if k == 1 or (k > 1 and k % 2 == 0):
@@ -193,25 +194,29 @@
             gates = jnp.concatenate([gates_all[s] for s in range(E)], axis=1).astype(jnp.float32)
             share = gates / jnp.sum(gates, axis=0, keepdims=True)
 
-        @pl.loop(0, experts)
-        def _(i, k=k):
-            part = project(k, i)
-            if k == 0:
-                acc[i] = part
-            elif k < T - 1:
-                acc[i] += part
-            else:
-                both = acc[i] + part
-                gate, up = both[:hidden_units], both[hidden_units:]
-                weight = jnp.sum(jnp.where(ids == e * experts + i, share, 0.0), axis=0, keepdims=True)
-                value = gate / (1.0 + jnp.exp(-gate)) * up * weight
-                hid_t[pl.ds(pl.multiple_of(i * hidden_units, hidden_units), hidden_units), :] = value
+        @pl.loop(0, experts // GROUP)
+        def _(step, k=k):
+            i = step * GROUP
+            parts = project(k, i).reshape(GROUP, 2 * hidden_units, -1)
+            for n in range(GROUP):
+                if k == 0:
+                    acc[i + n] = parts[n]
+                elif k < T - 1:
+                    acc[i + n] += parts[n]
+                else:
+                    both = acc[i + n] + parts[n]
+                    gate, up = both[:hidden_units], both[hidden_units:]
+                    weight = jnp.sum(jnp.where(ids == e * experts + i + n, share, 0.0), axis=0, keepdims=True)
+                    value = gate / (1.0 + jnp.exp(-gate)) * up * weight
+                    start = pl.multiple_of((i + n) * hidden_units, hidden_units)
+                    hid_t[pl.ds(start, hidden_units), :] = value
             if k + 2 < T:
-                for copy in weight_copies(k + 2, i):
-                    copy.start()
+                for n in range(GROUP):
+                    for copy in weight_copies(k + 2, i + n):
+                        copy.start()
             if k == 1:
-                for n in range(T * pieces // experts):
-                    j = i * (T * pieces // experts) + n
+                for n in range(GROUP * T * pieces // experts):
+                    j = step * (GROUP * T * pieces // experts) + n
                     order = lax.div(j, pieces)
                     down_copy((T - 1) - order, lax.rem(j, pieces)).start()
 
@@ -222,47 +227,47 @@
         start = pl.multiple_of(i * pair, pair)
         hid[:, pl.ds(start, pair)] = jnp.transpose(hid_t[pl.ds(start, pair), :]).astype(jnp.bfloat16)
 
-    width = min(256, feats)
-
-    def down_block(k, finish):
-        for piece in range(pieces):
-            down_copy(k, piece).wait()
-
-        @pl.loop(0, feats // width)
-        def _(n):
-            columns = pl.ds(pl.multiple_of(n * width, width), width)
-            finish(columns, jnp.dot(hid[...], down[k, :, columns], preferred_element_type=jnp.float32))
-
-    after_own = list(range(1, E)) + [0]
+    width = 256
+
+    parts_n = feats // width
+
+    def down_part(k, n):
+        if n == 0:
+            for piece in range(pieces):
+                down_copy(k, piece).wait()
+        return jnp.dot(
+            hid[...], down[k, :, n * width:(n + 1) * width], preferred_element_type=jnp.float32
+        )
+
+    def meet_partner(dx, n):
+        value = down_part(2 * dx, n)
+        arrived(from_partner.at[dx, n], p_send.at[dx, n], p_recv.at[dx, n])
+        return value + from_partner[dx, n].astype(jnp.float32)
+
     for dx in reversed(range(X)):
-        def keep(columns, value, dx=dx):
-            to_partner[dx, :, columns] = value.astype(jnp.bfloat16)
-
-        def store(columns, value):
-            own[:, columns] = value
-
-        down_block(2 * dx + 1, keep)
-        go(to_partner.at[dx], from_partner.at[dx], p_send.at[dx], p_recv.at[dx], (g, e, peer(1)))
-        down_block(2 * dx, store)
-        arrived(from_partner.at[dx], p_send.at[dx], p_recv.at[dx])
-        for j in after_own:
-            rows = rows_of(lax.rem(e + j, E))
-            total = own[rows, :] + from_partner[dx, rows, :].astype(jnp.float32)
-            if dx:
-                back = (X - dx) % X
-                to_x[dx, rows, :] = total.astype(jnp.bfloat16)
-                go(to_x.at[dx, rows, :], from_x.at[back, rows, :], x_send.at[dx, j], x_recv.at[back, j], (g, e, peer(2 * dx)))
-                continue
-            for other in range(1, X):
-                arrived(from_x.at[other, rows, :], x_send.at[other, j], x_recv.at[other, j])
-                total += from_x[other, rows, :].astype(jnp.float32)
-            if j:
-                to_z[j] = total.astype(jnp.bfloat16)
-                go(to_z.at[j], from_z.at[j], z_send.at[j], z_recv.at[j], (g, lax.rem(e + j, E), t))
-    for d in range(1, E):
-        arrived(from_z.at[d], z_send.at[d], z_recv.at[d])
-        total += from_z[d].astype(jnp.float32)
-    out_ref[...] = total.astype(out_ref.dtype)
+        for n in range(parts_n + 1):
+            if n < parts_n:
+                to_partner[dx, n] = down_part(2 * dx + 1, n).astype(jnp.bfloat16)
+                go(to_partner.at[dx, n], from_partner.at[dx, n], p_send.at[dx, n], p_recv.at[dx, n], (g, e, peer(1)))
+            if n and dx:
+                back, m = (X - dx) % X, n - 1
+                to_x[dx, m] = meet_partner(dx, m).astype(jnp.bfloat16)
+                go(to_x.at[dx, m], from_x.at[back, m], x_send.at[dx, m], x_recv.at[back, m], (g, e, peer(2 * dx)))
+            elif n:
+                own[n - 1] = meet_partner(0, n - 1)
+    for n in range(parts_n):
+        for other in range(1, X):
+            arrived(from_x.at[other, n], x_send.at[other, n], x_recv.at[other, n])
+            own[n] += from_x[other, n].astype(jnp.float32)
+        for j in range(1, E):
+            to_z[j, n] = own[n, rows_of(lax.rem(e + j, E)), :].astype(jnp.bfloat16)
+            go(to_z.at[j, n], from_z.at[j, n], z_send.at[j, n], z_recv.at[j, n], (g, lax.rem(e + j, E), t))
+    for n in range(parts_n):
+        total = own[n, rows_of(e), :]
+        for d in range(1, E):
+            arrived(from_z.at[d, n], z_send.at[d, n], z_recv.at[d, n])
+            total += from_z[d, n].astype(jnp.float32)
+        out_ref[:, n * width:(n + 1) * width] = total.astype(out_ref.dtype)
     for copy in sent:
         copy.wait_send()
 
@@ -273,6 +278,7 @@
 
 def scratch_of(tok_rows, feats, experts, hidden_units, E, T, per_token):
     bf16, f32, X, N = jnp.bfloat16, jnp.float32, T // 2, E * tok_rows
+    width, parts_n = 256, feats // 256
     dma = pltpu.SemaphoreType.DMA
     return [
         ((2 * experts, 2 * hidden_units, feats), bf16),
@@ -283,23 +289,23 @@
         ((experts, 2 * hidden_units, N), f32),
         ((experts * hidden_units, N), f32),
         ((N, experts * hidden_units), bf16),
-        ((X, N, feats), bf16),
-        ((X, N, feats), bf16),
-        ((X, N, feats), bf16),
-        ((X, N, feats), bf16),
-        ((E, tok_rows, feats), bf16),
-        ((E, tok_rows, feats), bf16),
-        ((N, feats), f32),
+        ((X, parts_n, N, width), bf16),
+        ((X, parts_n, N, width), bf16),
+        ((X, parts_n, N, width), bf16),
+        ((X, parts_n, N, width), bf16),
+        ((E, parts_n, tok_rows, width), bf16),
+        ((E, parts_n, tok_rows, width), bf16),
+        ((parts_n, N, width), f32),
     ], [
         dma((2 * experts, 2)), dma((T, down_pieces(experts, hidden_units))), dma((3,)),
         dma((E,)), dma((E,)), dma((2, E)), dma((2, E)), dma((T, E)), dma((T, E)),
-        dma((X,)), dma((X,)), dma((X, E)), dma((X, E)), dma((E,)), dma((E,)),
+        dma((X, parts_n)), dma((X, parts_n)), dma((X, parts_n)), dma((X, parts_n)), dma((E, parts_n)), dma((E, parts_n)),
     ]
 
 
 def fits_fused(sizes):
     tok_rows, feats, experts, hidden_units, E, T, per_token = sizes
-    if T % 2 or experts % 4 or E * tok_rows % 128 or feats % 256 or tok_rows % 16:
+    if T % 2 or experts % GROUP or experts % 4 or E * tok_rows % 128 or feats % 256 or tok_rows % 16:
         return False
     if 2 * hidden_units % 128 or hidden_units % 16 or T * 4 % experts:
         return False
@@ -325,7 +331,7 @@
     return pl.pallas_call(
         functools.partial(fused_kernel, *sizes[:6]),
         out_shape=jax.ShapeDtypeStruct(tokens.shape, tokens.dtype),
-        in_specs=[vmem, vmem, vmem, anywhere, anywhere, anywhere],
+        in_specs=[anywhere] * 6,
         out_specs=vmem,
         scratch_shapes=[pltpu.VMEM(shape, kind) for shape, kind in buffers] + semaphores,
         compiler_params=pltpu.CompilerParams(

time: 56.1 us -> 52.5 us (0.936)
  Pallas kernels: 54.4 us -> 50.9 us
    pallas_call x1, Pallas kernels: 54.4 us -> 50.9 us  [on_device(): pl.pallas_call(functools.partial(fused_kernel, *sizes[:6]), out_shape=jax...]
where the time goes in v2:
time: 52.5 us; the launch traced here: 52.4 us
  Pallas kernels  50.9 us (97%)
  local copies, waits for them, and re-layouts  1.47 us (3%)
    pallas_call x1, Pallas kernels, on_device(): pl.pallas_call(functools.partial(fused_kernel, *sizes[:6]), out_shape=jax...  50.9 us
    unnamed x1, local copies, waits for them, and re-layouts  1.47 us

profile of v2, /device:TPU:0, one launch (start us, length us, event | category | flops | bytes accessed | tf_op | source)
XLA Modules:
  0.0 52.4 jit_solution(12190839959787516674)
XLA Ops:
  0.0 50.9 %shard_map.64 = bf16[32,1024]{1,0:T(8,128)(2,1)} custom-call(bf16[32,1024]{1,0:T(8,128)(2,1)} %x_ref.1, s32[8,32]{1,0:T(8,128)} %bitcast.8, s32[8,32]{1,0:T(8,128)} %bitcast.9, bf16[16,192,4096]{2,1,0:T(8,128)(2,1)} %bitcast.5, bf16[16,192,4096]{2,1,0:T(8,128)(2,1)} %bitcast.6, bf16[3072,4096]{1,0:T(8,128)(2,1)} %bitcast.7), custom_call_target="tpu_custom_call" | custom-call | tf_op jit(solution)/shard_map/pallas_call | solution.py:331
  50.9 1.5 %copy.8 = bf16[32,1024]{1,0:T(8,128)(2,1)} copy(bf16[32,1024]{1,0:T(8,128)(2,1)} %shard_map.64) | data formatting | bytes 131072
